TPU v7x, 256 devices: a whole 4x4x8 slice. The times are simulated.
256 devices in a mesh: dp: 8 (over x, y_lo), expert: 16 (over z, core), tensor: 2 (over y_hi).
Axes of the slice: x: 4, y: 4 (y_hi: 2, y_lo: 2; y = y_hi * 2 + y_lo), z: 8, core: 2. Of those that a mesh axis runs over, the one named last changes fastest.
Arguments:
- tokens: bfloat16 [1536, 256, 1280], P(('dp', 'expert', 'tensor')), may hold values from -16 to 16
- cotangent: bfloat16 [1536, 256, 1280], P(('dp', 'expert', 'tensor')), may hold values from -6 to 6
- norm_gain: float32 [1280], replicated, may hold values from 0.5 to 1.5
- slot_keys: bfloat16 [1280, 32], replicated, may hold values from -2 to 2
- w_in: bfloat16 [16, 1280, 2560], P('expert', None, 'tensor'), may hold values from -0.15625 to 0.15625
- w_out: bfloat16 [16, 2560, 1280], P('expert', 'tensor'), may hold values from -0.125 to 0.125
Outputs:
- grad_tokens: bfloat16 [1536, 256, 1280], P(('dp', 'expert', 'tensor'))
- grad_gain: float32 [1280], replicated
- grad_keys: float32 [1280, 32], replicated
- grad_in: bfloat16 [16, 1280, 2560], P('expert', 'dp', 'tensor')
- grad_out: bfloat16 [16, 2560, 1280], P('expert', 'tensor', 'dp')
All inputs are finite; a program needn't handle non-finite values.
Results may differ from a plain program's by a relative error of at most 0.014.
The roundings to bfloat16 on the way count: a program that leaves them out, or rounds other values in their place, can miss the bound.
Values may be sent and summed in bfloat16 or wider, within the bound.
A program may use at most 128 MiB of HBM per device.

v0:
```python
import jax
import jax.numpy as jnp
from jax import lax
from jax.sharding import PartitionSpec as P

SLOT_PER = 2


EPSILON = 1e-06


def from_everyone(shard, axis):
    devices = lax.axis_size(axis)
    return lax.all_to_all(
        jnp.broadcast_to(shard[None], (devices, *shard.shape)), axis, 0, 0, tiled=True
    )


def in_order(tiles, dim):
    shape = list(tiles.shape[1:])
    shape[dim] *= tiles.shape[0]
    return jnp.moveaxis(tiles, 0, dim).reshape(shape)


def collect(shard, axis, dim):
    tiles = from_everyone(shard, axis)
    return in_order(tiles, dim)


def in_blocks(shard, dim, devices):
    before, after = (shard.shape[:dim], shard.shape[dim + 1 :])
    return jnp.moveaxis(shard.reshape(*before, devices, -1, *after), dim, 0)


def summed_on_arrival(shard, axis, dim):
    tiles = in_blocks(shard, dim, lax.axis_size(axis))
    arrived = lax.all_to_all(tiles, axis, split_axis=0, concat_axis=0, tiled=True)
    return arrived.sum(axis=0)


def sent_and_summed(shard, axis, dim):
    devices = lax.axis_size(axis)
    tiles = lax.all_to_all(in_blocks(shard, dim, devices), axis, 0, 0, tiled=True)
    return jnp.sum(tiles.astype(jnp.float32), axis=0)


def mixing_forward(tokens, gain, slot_keys):
    average = jnp.mean(tokens, axis=-1, keepdims=True, dtype=jnp.float32)
    centred = tokens.astype(jnp.float32) - average
    spread = jnp.mean(centred * centred, axis=-1, keepdims=True)
    inverse = lax.rsqrt(spread + EPSILON)
    scaled = centred * inverse
    normed = (scaled * gain).astype(jnp.bfloat16)
    logits = jnp.einsum("bmd,dn->bmn", normed, slot_keys, preferred_element_type=jnp.float32)
    dispatch = jax.nn.softmax(logits, axis=1)
    combine = jax.nn.softmax(logits, axis=2)
    dispatch_low = dispatch.astype(jnp.bfloat16)
    slot_values = jnp.einsum(
        "bmn,bmd->bnd", dispatch_low, normed, preferred_element_type=jnp.float32
    )
    return (slot_values, combine, (scaled, inverse, normed, dispatch, combine, dispatch_low))


def mixing_backward(saved, gain, slot_keys, slot_grad, combine_grad):
    scaled, inverse, normed, dispatch, combine, dispatch_low = saved
    grad_dispatch = jnp.einsum(
        "bnd,bmd->bmn", slot_grad, normed, preferred_element_type=jnp.float32
    )
    grad_normed = jnp.einsum(
        "bmn,bnd->bmd", dispatch_low, slot_grad, preferred_element_type=jnp.float32
    )
    grad_logits = dispatch * (
        grad_dispatch - jnp.sum(dispatch * grad_dispatch, axis=1, keepdims=True)
    )
    grad_logits = grad_logits + combine * (
        combine_grad - jnp.sum(combine * combine_grad, axis=2, keepdims=True)
    )
    keys_wide = slot_keys.astype(jnp.float32)
    grad_normed = grad_normed + jnp.einsum(
        "bmn,dn->bmd", grad_logits, keys_wide, precision=lax.Precision.HIGHEST
    )
    keys_term = jnp.einsum(
        "bmd,bmn->dn", normed.astype(jnp.float32), grad_logits, precision=lax.Precision.HIGHEST
    )
    gain_term = jnp.sum(grad_normed * scaled, axis=(0, 1))
    grad_scaled = grad_normed * gain
    first_mean = jnp.mean(grad_scaled, axis=-1, keepdims=True)
    second_mean = jnp.mean(grad_scaled * scaled, axis=-1, keepdims=True)
    grad_tok = inverse * (grad_scaled - first_mean - scaled * second_mean)
    return (grad_tok, gain_term, keys_term)


def contract_rows(left, right):
    return lax.dot_general(
        left, right, (((0,), (0,)), ((), ())), preferred_element_type=jnp.float32
    )


def contract_cols(left, right):
    return lax.dot_general(
        left, right, (((1,), (1,)), ((), ())), preferred_element_type=jnp.float32
    )


def local(tokens, cotangent, norm_gain, slot_keys, w_in, w_out):
    local_imgs, token_count, features = tokens.shape
    slot_count = slot_keys.shape[1]
    experts = slot_count // SLOT_PER
    slot_values, combine, saved = mixing_forward(tokens, norm_gain, slot_keys)
    slot_inputs = slot_values.astype(jnp.bfloat16).reshape(local_imgs, experts, SLOT_PER, features)
    arrived = lax.all_to_all(slot_inputs, "expert", split_axis=1, concat_axis=0, tiled=True)
    slot_rows = collect(arrived, "tensor", 0).reshape(-1, features)
    first_proj = w_in[0]
    second_proj = w_out[0]
    pre_act = jnp.dot(slot_rows, first_proj, preferred_element_type=jnp.float32)
    hidden = jax.nn.gelu(pre_act).astype(jnp.bfloat16)
    segment = hidden
    outputs = summed_on_arrival(
        jnp.dot(segment, second_proj, preferred_element_type=jnp.float32), "tensor", 0
    )
    outputs = outputs.astype(jnp.bfloat16).reshape(arrived.shape)
    returned = lax.all_to_all(outputs, "expert", split_axis=0, concat_axis=1, tiled=True).reshape(
        local_imgs, slot_count, features
    )
    combine_low = combine.astype(jnp.bfloat16)
    grad_slots = jnp.einsum(
        "bmn,bmd->bnd", combine_low, cotangent, preferred_element_type=jnp.float32
    )
    grad_slots = grad_slots.astype(jnp.bfloat16).reshape(local_imgs, experts, SLOT_PER, features)
    grad_combine = jnp.einsum(
        "bmd,bnd->bmn", cotangent, returned, preferred_element_type=jnp.float32
    )
    grads_sent = lax.all_to_all(grad_slots, "expert", split_axis=1, concat_axis=0, tiled=True)
    grad_rows = collect(grads_sent, "tensor", 0).reshape(-1, features)
    grad_hidden = contract_cols(grad_rows, second_proj)
    grad_pre = jax.vjp(jax.nn.gelu, pre_act)[1](grad_hidden)[0].astype(jnp.bfloat16)
    segment = grad_pre
    grad_in_rows = sent_and_summed(
        contract_cols(segment, first_proj).astype(jnp.bfloat16), "tensor", 0
    )
    grad_in_rows = grad_in_rows.astype(jnp.bfloat16).reshape(arrived.shape)
    grad_back = lax.all_to_all(
        grad_in_rows, "expert", split_axis=0, concat_axis=1, tiled=True
    ).reshape(local_imgs, slot_count, features)
    grad_tok, gain_term, keys_term = mixing_backward(
        saved, norm_gain, slot_keys, grad_back, grad_combine
    )
    grad_tokens = (cotangent.astype(jnp.float32) + grad_tok).astype(jnp.bfloat16)
    grad_gain, grad_keys = lax.psum((gain_term, keys_term), ("dp", "expert", "tensor"))
    columns = slot_rows
    grad_first = lax.psum_scatter(
        contract_rows(columns, grad_pre).astype(jnp.bfloat16), "dp", scatter_dimension=0, tiled=True
    )
    columns = grad_rows
    grad_second = (
        lax.psum_scatter(
            contract_rows(columns, hidden).astype(jnp.bfloat16),
            "dp",
            scatter_dimension=0,
            tiled=True,
        )
        .astype(jnp.float32)
        .T
    )
    return (
        grad_tokens,
        grad_gain,
        grad_keys,
        grad_first[None],
        grad_second.astype(jnp.bfloat16)[None],
    )


def solution(mesh):
    placed = (
        P(("dp", "expert", "tensor"), None, None),
        P(("dp", "expert", "tensor"), None, None),
        P(),
        P(),
        P("expert", None, "tensor"),
        P("expert", "tensor", None),
    )
    return jax.shard_map(
        local,
        mesh=mesh,
        in_specs=placed,
        out_specs=(
            P(("dp", "expert", "tensor"), None, None),
            P(),
            P(),
            P("expert", "dp", "tensor"),
            P("expert", "tensor", "dp"),
        ),
        check_vma=False,
    )
```

profile of v0, /device:TPU:1, one launch (start us, length us, event | category | flops | bytes accessed | tf_op | source)
XLA Modules:
  0.0 502.3 jit_solution(15583305845671244630)
XLA Ops:
  15.5 3.8 convolution_convert_fusion.3
  23.5 10.0 %all-to-all-start = ((bf16[6,16,2,1280]{3,2,0,1:T(2,128)(2,1)}), bf16[6,16,2,1280]{3,2,0,1:T(2,128)(2,1)}, u32[]{:S(2)}, u32[]{:S(2)}) async-start(bf16[6,16,2,1280]{3,2,0,1:T(2,128)(2,1)} %copy.15), calls=%async_computation | async-start | bytes 983040 | tf_op jit(solution)/shard_map/all_to_all | solution.py:133
  35.2 4.6 convolution_convert_fusion.2
  44.0 6.1 %all-to-all-done = bf16[6,16,2,1280]{3,2,0,1:T(2,128)(2,1)} async-done(((bf16[6,16,2,1280]{3,2,0,1:T(2,128)(2,1)}), bf16[6,16,2,1280]{3,2,0,1:T(2,128)(2,1)}, u32[]{:S(2)}, u32[]{:S(2)}) %all-to-all-start) | async-done | bytes 491552 | tf_op jit(solution)/shard_map/all_to_all | solution.py:133
  50.1 19.4 %all_to_all.80 = bf16[6,16,2,1280]{3,2,0,1:T(2,128)(2,1)S(1)} all-to-all(bf16[6,16,2,1280]{3,2,0,1:T(2,128)(2,1)} %copy.16), channel_id=1, replica_groups=mesh['dp'=8,'expert'=16,'tensor'=2] {'expert'}, dimensions={1} | all-to-all | bytes 983040 | tf_op jit(solution)/shard_map/all_to_all | solution.py:111
  70.0 18.9 %all_to_all.81 = bf16[2,96,1,2,1280]{4,3,2,1,0:T(2,128)(2,1)} all-to-all(bf16[2,96,1,2,1280]{4,3,2,1,0:T(2,128)(2,1)S(1)} %broadcast_in_dim.15), channel_id=1, replica_groups=mesh['dp'=8,'expert'=16,'tensor'=2] {'tensor'}, dimensions={0} | all-to-all | bytes 1966080 | tf_op jit(solution)/shard_map/all_to_all | solution.py:14
  91.4 4.6 all-to-all-start.1
  99.3 4.4 multiply_convert_fusion
  103.7 6.3 %all-to-all-done.1 = bf16[2,96,1,2,1280]{4,3,2,1,0:T(2,128)(2,1)} async-done(((bf16[2,96,1,2,1280]{4,3,2,1,0:T(2,128)(2,1)}), bf16[2,96,1,2,1280]{4,3,2,1,0:T(2,128)(2,1)}, u32[]{:S(2)}, u32[]{:S(2)}) %all-to-all-start.1) | async-done | bytes 983072 | tf_op jit(solution)/shard_map/all_to_all | solution.py:14
  113.3 4.9 fusion.33
  124.2 4.9 fusion.16
  129.2 8.3 %all-to-all-done.4 = bf16[2,192,1280]{2,1,0:T(8,128)(2,1)S(1)} async-done(((bf16[2,192,1280]{2,1,0:T(8,128)(2,1)}), bf16[2,192,1280]{2,1,0:T(8,128)(2,1)S(1)}, u32[]{:S(2)}, u32[]{:S(2)}) %all-to-all-start.4) | async-done | bytes 983072 | tf_op jit(solution)/shard_map/all_to_all | solution.py:43
  137.5 3.7 all-to-all-start.6
  144.3 19.8 %all-to-all-done.6 = f32[2,192,1280]{2,1,0:T(8,128)S(1)} async-done(((f32[2,192,1280]{2,1,0:T(8,128)}), f32[2,192,1280]{2,1,0:T(8,128)S(1)}, u32[]{:S(2)}, u32[]{:S(2)}) %all-to-all-start.6) | async-done | bytes 1966112 | tf_op jit(solution)/shard_map/all_to_all | solution.py:37
  164.1 6.3 %all-to-all-start.5 = ((bf16[96,1,2,1280]{3,2,1,0:T(2,128)(2,1)}), bf16[96,1,2,1280]{3,2,1,0:T(2,128)(2,1)S(1)}, u32[]{:S(2)}, u32[]{:S(2)}) async-start(bf16[96,1,2,1280]{3,2,1,0:T(2,128)(2,1)} %reshape.82), calls=%async_computation.5 | async-start | bytes 983040 | tf_op jit(solution)/shard_map/all_to_all | solution.py:142
  171.5 15.6 %all-to-all-done.5 = bf16[96,1,2,1280]{3,2,1,0:T(2,128)(2,1)S(1)} async-done(((bf16[96,1,2,1280]{3,2,1,0:T(2,128)(2,1)}), bf16[96,1,2,1280]{3,2,1,0:T(2,128)(2,1)S(1)}, u32[]{:S(2)}, u32[]{:S(2)}) %all-to-all-start.5) | async-done | bytes 491552 | tf_op jit(solution)/shard_map/all_to_all | solution.py:142
  194.8 11.7 %all-to-all-done.7 = bf16[96,1,2,1280]{3,2,1,0:T(2,128)(2,1)S(1)} async-done(((bf16[96,1,2,1280]{3,2,1,0:T(2,128)(2,1)}), bf16[96,1,2,1280]{3,2,1,0:T(2,128)(2,1)S(1)}, u32[]{:S(2)}, u32[]{:S(2)}) %all-to-all-start.7) | async-done | bytes 491552 | tf_op jit(solution)/shard_map/all_to_all | solution.py:122
  213.7 5.0 convolution_convert_fusion.1
  219.0 4.9 convolution_convert_fusion
  224.0 5.6 %fusion.44 = f32[6,256,1280]{2,1,0:T(8,128)} fusion(bf16[6,32,1280]{2,1,0:T(8,128)(2,1)S(1)} %reshape.83, f32[6,32]{1,0:T(8,128)S(1)} %get-tuple-element.8, f32[6,256,32]{1,2,0:T(8,128)} %copy-done.4), kind=kOutput, calls=%fused_computation.58 | convolution fusion | flops 125977024 | bytes 8553216 | tf_op jit(solution)/shard_map/bmn,bnd->bmd/dot_general | solution.py:69
  229.6 10.7 %fusion.14 = (f32[1280]{0:T(1024)S(1)}, f32[6,256]{1,0:T(8,128)S(1)}, f32[6,256]{1,0:T(8,128)S(1)}, f32[6,256,1280]{2,1,0:T(8,128)}) fusion(bf16[6,256,1280]{2,1,0:T(8,128)(2,1)} %param.6, f32[6,256]{1,0:T(8,128)S(1)} %add_rsqrt_fusion, f32[6,256]{1,0:T(8,128)S(1)} %broadcast_multiply_fusion.2, f32[1280]{0:T(1024)S(1)} %copy-done.10, ...), kind=kOutput, calls=%fused_computation.16 | convolution fusion | flops 774631168 | bytes 19974144 | tf_op jit(solution)/shard_map/bmn,dn->bmd/dot_general | solution.py:79
  240.2 79.7 %psum.14 = f32[1280]{0:T(1024)} all-reduce(f32[1280]{0:T(1024)S(1)} %get-tuple-element.5), channel_id=1, replica_groups=mesh['dp'=8,'expert'=16,'tensor'=2] {'dp','expert','tensor'}, use_global_device_ids=true, to_apply=%region_13.0 | all-reduce | flops 1280 | bytes 10240 | tf_op jit(solution)/shard_map/psum | solution.py:149
  319.9 8.7 %fusion.13 = bf16[6,256,1280]{2,1,0:T(8,128)(2,1)} fusion(bf16[6,256,1280]{2,1,0:T(8,128)(2,1)} %param.6, bf16[6,256,1280]{2,1,0:T(8,128)(2,1)} %param.7, f32[6,256,1280]{2,1,0:T(8,128)} %get-tuple-element.18, f32[6,256]{1,0:T(8,128)S(1)} %get-tuple-element.19, f32[6,256]{1,0:T(8,128)S(1)} %get-tuple-element.20, f32[1280]{0:T(1024)S(1)} %copy-done.10, ...), kind=kLoop, calls=%fused_computation.15 | loop fusion | flops 21626880 | bytes 19690496 | tf_op jit(solution)/shard_map/convert_element_type | solution.py:148
  328.6 164.7 %all-reduce.2.cloned.1.call-done = f32[1280,32]{0,1:T(8,128)} async-done(((f32[1280,32]{0,1:T(8,128)}), f32[1280,32]{0,1:T(8,128)}) %all-reduce.2.cloned.1.call-update) | async-done | bytes 163856 | tf_op jit(solution)/shard_map/psum | solution.py:149
  (64 shorter events, 54.1 us)
Async XLA Ops:
  8.0 91.3 %copy-start = (bf16[1,1280,1280]{2,1,0:T(8,128)(2,1)S(1)}, bf16[1,1280,1280]{2,1,0:T(8,128)(2,1)}, u32[]{:S(2)}) copy-start(bf16[1,1280,1280]{2,1,0:T(8,128)(2,1)} %param.10) | copy-start | bytes 9830404
  8.0 3.4 copy-start.2
  8.0 4.6 copy-start.10
  8.0 4.6 copy-start.8
  14.4 0.7 copy-start.4
  23.5 26.6 %all-to-all-start = ((bf16[6,16,2,1280]{3,2,0,1:T(2,128)(2,1)}), bf16[6,16,2,1280]{3,2,0,1:T(2,128)(2,1)}, u32[]{:S(2)}, u32[]{:S(2)}) async-start(bf16[6,16,2,1280]{3,2,0,1:T(2,128)(2,1)} %copy.15), calls=%async_computation | async-start | bytes 983040 | tf_op jit(solution)/shard_map/all_to_all | solution.py:133
  91.4 18.6 %all-to-all-start.1 = ((bf16[2,96,1,2,1280]{4,3,2,1,0:T(2,128)(2,1)}), bf16[2,96,1,2,1280]{4,3,2,1,0:T(2,128)(2,1)}, u32[]{:S(2)}, u32[]{:S(2)}) async-start(bf16[2,96,1,2,1280]{4,3,2,1,0:T(2,128)(2,1)} %broadcast_in_dim.13), calls=%async_computation.1 | async-start | bytes 1966080 | tf_op jit(solution)/shard_map/all_to_all | solution.py:14
  118.2 2.4 copy-start.11
  120.7 16.8 %all-to-all-start.4 = ((bf16[2,192,1280]{2,1,0:T(8,128)(2,1)}), bf16[2,192,1280]{2,1,0:T(8,128)(2,1)S(1)}, u32[]{:S(2)}, u32[]{:S(2)}) async-start(bf16[2,192,1280]{2,1,0:T(8,128)(2,1)} %bitcast.77), calls=%async_computation.4 | async-start | bytes 1966080 | tf_op jit(solution)/shard_map/all_to_all | solution.py:43
  137.5 26.6 %all-to-all-start.6 = ((f32[2,192,1280]{2,1,0:T(8,128)}), f32[2,192,1280]{2,1,0:T(8,128)S(1)}, u32[]{:S(2)}, u32[]{:S(2)}) async-start(f32[2,192,1280]{2,1,0:T(8,128)} %fusion.16), calls=%async_computation.6 | async-start | bytes 3932160 | tf_op jit(solution)/shard_map/all_to_all | solution.py:37
  144.3 47.1 %copy-start.7 = (f32[6,256,32]{1,2,0:T(8,128)S(1)}, f32[6,256,32]{1,2,0:T(8,128)}, u32[]{:S(2)}) copy-start(f32[6,256,32]{1,2,0:T(8,128)} %get-tuple-element.9) | copy-start | bytes 589828
  164.1 23.0 %all-to-all-start.5 = ((bf16[96,1,2,1280]{3,2,1,0:T(2,128)(2,1)}), bf16[96,1,2,1280]{3,2,1,0:T(2,128)(2,1)S(1)}, u32[]{:S(2)}, u32[]{:S(2)}) async-start(bf16[96,1,2,1280]{3,2,1,0:T(2,128)(2,1)} %reshape.82), calls=%async_computation.5 | async-start | bytes 983040 | tf_op jit(solution)/shard_map/all_to_all | solution.py:142
  187.1 19.4 %all-to-all-start.7 = ((bf16[96,1,2,1280]{3,2,1,0:T(2,128)(2,1)}), bf16[96,1,2,1280]{3,2,1,0:T(2,128)(2,1)S(1)}, u32[]{:S(2)}, u32[]{:S(2)}) async-start(bf16[96,1,2,1280]{3,2,1,0:T(2,128)(2,1)} %convert_element_type.73), calls=%async_computation.7 | async-start | bytes 983040 | tf_op jit(solution)/shard_map/all_to_all | solution.py:122
  190.5 302.7 %all-reduce.2.cloned.1.call-start = ((), (), s32[]{:S(2)}) async-start(), calls=%async_computation.10 | async-start | bytes 327680 | tf_op jit(solution)/shard_map/psum | solution.py:149
  207.0 3.7 copy-start.3
  210.7 3.0 copy-start.6
  213.6 5.4 %copy-start.5 = (bf16[384,1280]{1,0:T(8,128)(2,1)S(1)}, bf16[384,1280]{1,0:T(8,128)(2,1)}, u32[]{:S(2)}) copy-start(bf16[384,1280]{1,0:T(8,128)(2,1)} %reshape_reshape.6) | copy-start | bytes 2949124
  213.7 279.6 %reduce-scatter.3.cloned.1.call-start = ((), (), s32[]{:S(2)}) async-start(), calls=%async_computation.11 | async-start | bytes 3686400 | tf_op jit(solution)/shard_map/reduce_scatter | solution.py:151
  218.7 274.5 %reduce-scatter.5.cloned.1.call-start = ((), (), s32[]{:S(2)}) async-start(), calls=%async_computation.12 | async-start | bytes 3686400 | tf_op jit(solution)/shard_map/reduce_scatter | solution.py:156
  224.0 5.6 %copy-start.9 = (bf16[1280,32]{0,1:T(8,128)(2,1)S(1)}, bf16[1280,32]{0,1:T(8,128)(2,1)}, u32[]{:S(2)}) copy-start(bf16[1280,32]{0,1:T(8,128)(2,1)} %param.9) | copy-start | bytes 245764
  319.9 174.9 %copy-start.1 = (bf16[1,1280,1280]{2,1,0:T(8,128)(2,1)S(1)}, bf16[1,1280,1280]{2,1,0:T(8,128)(2,1)}, u32[]{:S(2)}) copy-start(bf16[1,1280,1280]{2,1,0:T(8,128)(2,1)} %param.10) | copy-start | bytes 9830404
Sparse Core Ops, SparseCore 0:
  213.8 279.4 all-reduce.1
Sparse Core Ops, SparseCore 1:
  218.8 71.0 reduce-scatter.2
  292.9 76.7 reduce-scatter.4
where the time goes:
time: 504 us; the launch traced here: 502 us
  waiting for transfers between devices  232 us (46%)
  blocking collectives  118 us (23%)
  matrix products  62.9 us (12%)
  starting transfers between devices  32.3 us (6%)
  local copies, waits for them, and re-layouts  24.8 us (5%)
  other arithmetic  16.2 us (3%)
  between operations  15.7 us (3%)
    psum x1, waiting for transfers between devices, local(): lax.psum((gain_term, keys_term), ('dp', 'expert', 'tensor'))  165 us
    psum x1, blocking collectives, local(): lax.psum((gain_term, keys_term), ('dp', 'expert', 'tensor'))  79.7 us
    all_to_all x1, waiting for transfers between devices, summed_on_arrival(): lax.all_to_all(tiles, axis, split_axis=0, concat_axis=0, tiled=True)  19.8 us
    all_to_all x1, blocking collectives, local(): lax.all_to_all(slot_inputs, 'expert', split_axis=1, concat_axis=0, tiled=...  19.4 us
    all_to_all x1, blocking collectives, from_everyone(): lax.all_to_all(jnp.broadcast_to(shard[None], (devices, *shard.shape)), ax...  18.9 us
    all_to_all x1, waiting for transfers between devices, local(): lax.all_to_all(grad_in_rows, 'expert', split_axis=0, concat_axis=1, tiled...  15.6 us
    all_to_all x1, waiting for transfers between devices, local(): lax.all_to_all(outputs, 'expert', split_axis=0, concat_axis=1, tiled=True)  11.7 us
    dot_general x1, matrix products, mixing_backward(): jnp.einsum('bmn,dn->bmd', grad_logits, keys_wide, precision=lax.Precision...  10.7 us
  transfers between devices with their start and end apart: 9, of which 7 were waited for; matrix products, arithmetic and copies ran while one was open for 13% of the time, Pallas kernels for 0%

commit v1 on v0

v1 whole, which is shorter than its diff:
```python
import functools
import math

import jax
import jax.numpy as jnp
from jax import lax
from jax.experimental import pallas as pl
from jax.experimental.pallas import tpu as pltpu
from jax.sharding import PartitionSpec as P

MESH = pl.DeviceIdType.MESH
EPSILON = 1e-06
F32 = jnp.float32
BF16 = jnp.bfloat16

IMGS = 6
BATCHES = 3
TOK = 256
D = 1280
SLOTS = 32
EXP = 16
HID = 1280
ROWS = 384
HALF = 640
NT = (((1,), (1,)), ((), ()))
TN = (((0,), (0,)), ((), ()))
OWNERS = 10
STAT = 40
CHUNK = 32


def dot(a, b, dims=(((1,), (0,)), ((), ()))):
    return lax.dot_general(a, b, dims, preferred_element_type=F32)


def to_blocks():
    r = lax.broadcasted_iota(jnp.int32, (128, 128), 0)
    c = lax.broadcasted_iota(jnp.int32, (128, 128), 1)
    want = ((r >> 2) & 1) * 64 + ((r >> 1) & 1) * 32 + (r >> 3) * 2 + (r & 1)
    return jnp.where(c == want, 1.0, 0.0).astype(BF16)


def to_blocks_inverse():
    r = lax.broadcasted_iota(jnp.int32, (128, 128), 0)
    c = lax.broadcasted_iota(jnp.int32, (128, 128), 1)
    want = ((c >> 2) & 1) * 64 + ((c >> 1) & 1) * 32 + (c >> 3) * 2 + (c & 1)
    return jnp.where(r == want, 1.0, 0.0).astype(BF16)


def to_kinds():
    r = lax.broadcasted_iota(jnp.int32, (128, 128), 0)
    c = lax.broadcasted_iota(jnp.int32, (128, 128), 1)
    want = ((r >> 2) & 15) * 8 + (r >> 6) * 4 + (r & 3)
    return jnp.where(c == want, 1.0, 0.0).astype(BF16)


def to_kinds_inverse():
    r = lax.broadcasted_iota(jnp.int32, (128, 128), 0)
    c = lax.broadcasted_iota(jnp.int32, (128, 128), 1)
    want = ((c >> 2) & 15) * 8 + (c >> 6) * 4 + (c & 3)
    return jnp.where(r == want, 1.0, 0.0).astype(BF16)


def nth_offset(j):
    half = lax.div(j, 2)
    return jnp.where(lax.rem(j, 2) == 0, half + 1, 15 - half)


def kernel(
    tok_hbm, cot_hbm, gain_ref, keys_ref, win_hbm, wout_hbm,
    out_hbm, fin_ref, g1_ref, g2_ref,
    tok, cot, normed, win, wout, disp, comb, stat, stage, sendbuf, rbuf,
    srows, grows, srows_t, grows_t, hidden, gpre, psend, precv, own, rsend, rback,
    p1, p2, a1p, a1m, a2p, a2m, a3p, a3m, ya, yb, tb, b1p, b1m, b2p, b2m, b3p, b3m, ysum,
    gn, both, acc, gacc, ar_a, ar_x, ar_y,
    tok_sem, cot_sem, w_sem, out_sem, own_sem,
    as_sem, ar_sem, fs_sem, fr_sem, ps_sem, pr_sem, bs_sem, br_sem,
    ras_sem, rar_sem, rbs_sem, rbr_sem, yas_sem, yar_sem, ybs_sem, ybr_sem,
    ra_s, ra_r, rx_s, rx_r, ry_s, ry_r, rc_s, rc_r,
):
    dp = lax.axis_index("dp")
    e = lax.axis_index("expert")
    t = lax.axis_index("tensor")
    x = lax.div(dp, 2)
    ylo = lax.rem(dp, 2)
    y = t * 2 + ylo
    partner = (dp + 1 - 2 * ylo, e, 1 - t)
    ypeer = (dp + 1 - 2 * ylo, e, t)
    xp1 = lax.rem(x + 1, 4)
    xm1 = lax.rem(x + 3, 4)
    xp2 = lax.rem(x + 2, 4)
    xplus = (xp1 * 2 + ylo, e, t)
    xminus = (xm1 * 2 + ylo, e, t)

    def remote(src, dst, s, r, dev):
        return pltpu.make_async_remote_copy(
            src_ref=src, dst_ref=dst, send_sem=s, recv_sem=r, device_id=dev, device_id_type=MESH
        )

    def xdev(k):
        return (lax.rem(x + k, 4) * 2 + ylo, e, t)

    def ydev(k):
        yy = lax.rem(y + k, 4)
        return (x * 2 + lax.rem(yy, 2), e, lax.div(yy, 2))

    def load(i, c):
        pltpu.make_async_copy(tok_hbm.at[i], tok.at[i], tok_sem.at[i]).start()
        pltpu.make_async_copy(cot_hbm.at[i], cot.at[i], cot_sem.at[i]).start()
        return c

    lax.fori_loop(0, IMGS, load, 0)
    pltpu.make_async_copy(win_hbm.at[0], win, w_sem.at[0]).start()
    pltpu.make_async_copy(wout_hbm.at[0], wout, w_sem.at[1]).start()

    barrier = pltpu.get_barrier_semaphore()

    def greet(k, c):
        pl.semaphore_signal(
            barrier, inc=1, device_id=(dp, lax.rem(e + k, EXP), t), device_id_type=MESH
        )
        return c

    lax.fori_loop(1, EXP, greet, 0)
    for k in (1, 2, 3):
        pl.semaphore_signal(barrier, inc=1, device_id=xdev(k), device_id_type=MESH)
        pl.semaphore_signal(barrier, inc=1, device_id=ydev(k), device_id_type=MESH)

    def forward_image(i, row):
        pltpu.make_async_copy(tok_hbm.at[i], tok.at[i], tok_sem.at[i]).wait()

        def norm_rows(r, c):
            rows = pl.ds(pl.multiple_of(r * CHUNK, CHUNK), CHUNK)
            v = tok[i, rows, :].astype(F32)
            mean = jnp.mean(v, axis=-1, keepdims=True)
            centred = v - mean
            inv = lax.rsqrt(jnp.mean(centred * centred, axis=-1, keepdims=True) + EPSILON)
            stat[i, rows, 0:1] = mean
            stat[i, rows, 1:2] = inv
            normed[i, rows, :] = (centred * inv * gain_ref[...]).astype(BF16)
            return c

        lax.fori_loop(0, TOK // CHUNK, norm_rows, 0)
        logits = dot(keys_ref[...], normed[i], NT)
        shifted = jnp.exp(logits - jnp.max(logits, axis=1, keepdims=True))
        dis = shifted / jnp.sum(shifted, axis=1, keepdims=True)
        raised = jnp.exp(logits - jnp.max(logits, axis=0, keepdims=True))
        com = raised / jnp.sum(raised, axis=0, keepdims=True)
        disp[i] = dis
        comb[i] = com
        here = pl.multiple_of(row * SLOTS, SLOTS)
        stage[pl.ds(here, SLOTS), :] = dot(dis.astype(BF16), normed[i]).astype(BF16)
        pltpu.make_async_copy(cot_hbm.at[i], cot.at[i], cot_sem.at[i]).wait()
        stage[pl.ds(here + 64, SLOTS), :] = dot(com.astype(BF16), cot[i]).astype(BF16)

    def a2a(b, j):
        k = nth_offset(j)
        to = lax.rem(e + k, EXP)
        return remote(
            sendbuf.at[pl.ds(pl.multiple_of(b * 128 + to * 8, 8), 8)],
            rbuf.at[pl.ds(pl.multiple_of(b * 128 + e * 8, 8), 8)],
            as_sem.at[b, j], ar_sem.at[b, j], (dp, to, t),
        )

    def own_copy(b):
        return pltpu.make_async_copy(
            sendbuf.at[pl.ds(pl.multiple_of(b * 128 + e * 8, 8), 8)],
            rbuf.at[pl.ds(pl.multiple_of(b * 128 + e * 8, 8), 8)],
            own_sem.at[b],
        )

    for b in range(BATCHES):

        def image(i, c, b=b):
            forward_image(2 * b + i, i)
            return c

        lax.fori_loop(0, 2, image, 0)
        sendbuf[pl.ds(b * 128, 128), :] = dot(to_blocks(), stage[...]).astype(BF16)
        if b == 0:
            pl.semaphore_wait(barrier, 21)
        own_copy(b).start()

        def send(j, c, b=b):
            a2a(b, j).start()
            return c

        lax.fori_loop(0, 15, send, 0)

    def relay(b, src, n):
        at = pl.multiple_of(b * 128 + src * 8, 8)
        return remote(
            rbuf.at[pl.ds(at, 8)],
            rbuf.at[pl.ds(at + ROWS, 8)],
            fs_sem.at[b, n], fr_sem.at[b, n], partner,
        )

    for b in range(BATCHES):
        own_copy(b).wait()
        relay(b, e, 15).start()

        def forward(j, c, b=b):
            a2a(b, j).wait_recv()
            src = lax.rem(e + EXP - nth_offset(j), EXP)
            relay(b, src, j).start()
            return c

        lax.fori_loop(0, 15, forward, 0)

    for i in range(2):
        pltpu.make_async_copy((win_hbm, wout_hbm)[i].at[0], (win, wout)[i], w_sem.at[i]).wait()

    def arrived(b, c):
        def one(n, c):
            relay(b, e, n).wait_recv()
            return c

        return lax.fori_loop(0, 16, one, c)

    lax.fori_loop(0, BATCHES, arrived, 0)

    def split(b, c):
        v = dot(to_kinds(), rbuf[pl.ds(pl.multiple_of(b * 128, 128), 128), :]).astype(BF16)
        at = pl.ds(pl.multiple_of(b * 64, 64), 64)
        srows[at, :] = v[0:64]
        grows[at, :] = v[64:128]
        return c

    lax.fori_loop(0, 6, split, 0)

    root = math.sqrt(2.0 / math.pi)

    def middle(n, c):
        cols = pl.ds(pl.multiple_of(n * 256, 256), 256)
        pre = dot(srows[...], win[:, cols])
        gh = dot(grows[...], wout[cols, :], NT)
        square = pre * pre
        th = jnp.tanh(root * (pre + 0.044715 * (square * pre)))
        cdf = 0.5 * (1.0 + th)
        hidden[:, cols] = (pre * cdf).astype(BF16)
        slope = cdf + 0.5 * pre * (1.0 - th * th) * (root * (1.0 + 3.0 * 0.044715 * square))
        gpre[:, cols] = (gh * slope).astype(BF16)
        return c

    lax.fori_loop(0, 5, middle, 0)

    def theirs(n, c):
        cols = pl.ds(pl.multiple_of(n * 256, 256), 256)
        o = dot(hidden[192:384, :], wout[:, cols]).astype(BF16)
        g = dot(gpre[192:384, :], win[cols, :], NT).astype(BF16)
        for b in range(BATCHES):
            psend[b * 128 : b * 128 + 64, cols] = o[b * 64 : b * 64 + 64]
            psend[b * 128 + 64 : b * 128 + 128, cols] = g[b * 64 : b * 64 + 64]
        return c

    lax.fori_loop(0, 5, theirs, 0)

    def partial(b):
        at = pl.ds(b * 128, 128)
        return remote(psend.at[at], precv.at[at], ps_sem.at[b], pr_sem.at[b], partner)

    for b in range(BATCHES):
        partial(b).start()

    def ours(n, c):
        cols = pl.ds(pl.multiple_of(n * 256, 256), 256)
        o = dot(hidden[0:192, :], wout[:, cols])
        g = dot(gpre[0:192, :], win[cols, :], NT)
        for b in range(BATCHES):
            own[b * 128 : b * 128 + 64, cols] = o[b * 64 : b * 64 + 64]
            own[b * 128 + 64 : b * 128 + 128, cols] = g[b * 64 : b * 64 + 64]
        return c

    lax.fori_loop(0, 5, ours, 0)

    def turn(n, c):
        cols = pl.ds(pl.multiple_of(n * 128, 128), 128)
        srows_t[cols, :] = srows[:, cols].T
        grows_t[cols, :] = grows[:, cols].T
        return c

    lax.fori_loop(0, 10, turn, 0)

    lo = pl.ds(0, HALF)
    hi = pl.ds(HALF, HALF)

    def rows_a(k):
        return pl.ds(pl.multiple_of(k * 320, 320), 320)

    def rows_b(k, which):
        return pl.ds(pl.multiple_of(k * 320 + which * 160, 160), 160)

    def rows_t(k):
        return pl.ds(pl.multiple_of(k * 160, 160), 160)

    def ring(rows, buf, bufs, s, r):
        one_p, one_m, two_p, two_m, three_p, three_m = bufs
        return dict(
            far_p=remote(buf.at[rows(xp2), lo], one_p, s.at[0], r.at[0], xplus),
            far_m=remote(buf.at[rows(xp2), hi], one_m, s.at[1], r.at[1], xminus),
            raw_p=remote(buf.at[rows(xp1), hi], three_p, s.at[2], r.at[2], xplus),
            raw_m=remote(buf.at[rows(xm1), lo], three_m, s.at[3], r.at[3], xminus),
            sum_p=remote(one_p, two_p, s.at[4], r.at[4], xplus),
            sum_m=remote(one_m, two_m, s.at[5], r.at[5], xminus),
        )

    ring_a = ring(rows_a, p1, (a1p, a1m, a2p, a2m, a3p, a3m), ras_sem, rar_sem)
    ring_b = ring(rows_t, tb, (b1p, b1m, b2p, b2m, b3p, b3m), rbs_sem, rbr_sem)

    def send_y(q, k):
        return remote(p2.at[rows_b(k, 1 - ylo)], yb.at[rows_t(k)], ybs_sem.at[q], ybr_sem.at[q], ypeer)

    chunks = (xp2, xp1, xm1, x)
    for q, k in enumerate(chunks):

        def grads(n, c, k=k):
            cols = pl.ds(pl.multiple_of(n * 256, 256), 256)
            p1[rows_a(k), cols] = dot(srows_t[rows_a(k), :], gpre[:, cols]).astype(BF16)
            p2[rows_a(k), cols] = dot(grows_t[rows_a(k), :], hidden[:, cols]).astype(BF16)
            return c

        lax.fori_loop(0, 5, grads, 0)
        send_y(q, k).start()
        if q == 0:
            ring_a["far_p"].start()
            ring_a["far_m"].start()
        elif q == 1:
            ring_a["raw_p"].start()
        elif q == 2:
            ring_a["raw_m"].start()

    def back(b, j):
        k = nth_offset(j)
        to = lax.rem(e + k, EXP)
        return remote(
            rsend.at[pl.ds(pl.multiple_of(b * 128 + to * 8, 8), 8)],
            rback.at[pl.ds(pl.multiple_of(b * 128 + e * 8, 8), 8)],
            bs_sem.at[b, j], br_sem.at[b, j], (dp, to, t),
        )

    def own_back(b):
        return pltpu.make_async_copy(
            rsend.at[pl.ds(pl.multiple_of(b * 128 + e * 8, 8), 8)],
            rback.at[pl.ds(pl.multiple_of(b * 128 + e * 8, 8), 8)],
            own_sem.at[b],
        )

    def give_back(b):
        at = pl.ds(b * 128, 128)
        partial(b).wait_recv()
        whole = (own[at, :] + precv[at, :].astype(F32)).astype(BF16)
        rsend[at, :] = dot(to_kinds_inverse(), whole).astype(BF16)
        own_back(b).start()

        def send(j, c):
            back(b, j).start()
            return c

        lax.fori_loop(0, 15, send, 0)

    def add_rows(dst, parts, count):
        def step(r, c):
            rows = pl.ds(pl.multiple_of(r * 32, 32), 32)
            total = parts[0](rows).astype(F32)
            for p in parts[1:]:
                total = total + p(rows).astype(F32)
            dst(rows, total.astype(BF16))
            return c

        lax.fori_loop(0, count // 32, step, 0)

    def pass_on(rg, buf, base, one_p, one_m, count):
        rg["far_p"].wait_recv()

        def put_p(rows, v):
            one_p[rows, :] = v

        add_rows(
            put_p,
            (lambda r: one_p[r, :], lambda r: buf[pl.ds(base(xp1) + r.start, 32), lo]),
            count,
        )
        rg["sum_p"].start()
        rg["far_m"].wait_recv()

        def put_m(rows, v):
            one_m[rows, :] = v

        add_rows(
            put_m,
            (lambda r: one_m[r, :], lambda r: buf[pl.ds(base(xm1) + r.start, 32), hi]),
            count,
        )
        rg["sum_m"].start()

    def base_a(k):
        return pl.multiple_of(k * 320, 32)

    def base_t(k):
        return pl.multiple_of(k * 160, 32)

    def take_y(q, k):
        send_y(q, k).wait_recv()

        def put(rows, v):
            tb[pl.ds(base_t(k) + rows.start, 32), :] = v

        add_rows(
            put,
            (
                lambda r: yb[pl.ds(base_t(k) + r.start, 32), :],
                lambda r: p2[pl.ds(pl.multiple_of(k * 320 + ylo * 160, 32) + r.start, 32), :],
            ),
            160,
        )

    give_back(0)
    pass_on(ring_a, p1, base_a, a1p, a1m, 320)
    take_y(0, xp2)
    ring_b["far_p"].start()
    ring_b["far_m"].start()
    give_back(1)
    take_y(1, xp1)
    ring_b["raw_p"].start()
    give_back(2)

    acc[...] = jnp.zeros_like(acc)
    gacc[...] = jnp.zeros_like(gacc)

    def backward_image(i, row):
        here = pl.multiple_of(row * SLOTS, SLOTS)
        outs = stage[pl.ds(here, SLOTS), :]
        gin = stage[pl.ds(here + 64, SLOTS), :]
        gc = dot(outs, cot[i], NT)
        gd = dot(gin, normed[i], NT)
        dis = disp[i]
        com = comb[i]
        gl = dis * (gd - jnp.sum(dis * gd, axis=1, keepdims=True))
        gl = gl + com * (gc - jnp.sum(com * gc, axis=0, keepdims=True))
        high = gl.astype(BF16)
        low = (gl - high.astype(F32)).astype(BF16)
        terms = jnp.concatenate([high, low], axis=0)
        kt = dot(terms, normed[i])
        acc[0:SLOTS, :] += kt[0:SLOTS] + kt[SLOTS : 2 * SLOTS]
        both[0:SLOTS, :] = gin
        left = jnp.concatenate([dis.astype(BF16), high, low], axis=0)
        gn[...] = dot(left, both[...], TN)

        def rows_of(r, c):
            rows = pl.ds(pl.multiple_of(r * CHUNK, CHUNK), CHUNK)
            mean = stat[i, rows, 0:1]
            inv = stat[i, rows, 1:2]
            g = gn[rows, :]
            scaled = (tok[i, rows, :].astype(F32) - mean) * inv
            prod = g * scaled
            gacc[...] += jnp.sum(prod.reshape(CHUNK // 8, 8, D), axis=0)
            gain = gain_ref[...]
            gs = g * gain
            m1 = jnp.mean(gs, axis=-1, keepdims=True)
            m2 = jnp.mean(prod * gain, axis=-1, keepdims=True)
            res = cot[i, rows, :].astype(F32) + inv * (gs - m1 - scaled * m2)
            normed[i, rows, :] = res.astype(BF16)
            return c

        lax.fori_loop(0, TOK // CHUNK, rows_of, 0)
        pltpu.make_async_copy(normed.at[i], out_hbm.at[i], out_sem.at[i]).start()

    both[SLOTS : 2 * SLOTS, :] = keys_ref[...]
    both[2 * SLOTS : 3 * SLOTS, :] = keys_ref[...]

    def backward_batch(b):
        own_back(b).wait()

        def one(j, c):
            back(b, j).wait_recv()
            return c

        lax.fori_loop(0, 15, one, 0)
        stage[...] = dot(to_blocks_inverse(), rback[pl.ds(b * 128, 128), :]).astype(BF16)

        def image(i, c):
            backward_image(2 * b + i, i)
            return c

        lax.fori_loop(0, 2, image, 0)

    backward_batch(0)
    take_y(2, xm1)
    ring_b["raw_m"].start()
    pass_on(ring_b, tb, base_t, b1p, b1m, 160)
    backward_batch(1)
    take_y(3, x)
    backward_batch(2)

    acc[SLOTS : SLOTS + 8, :] = jnp.sum(gacc[...], axis=0, keepdims=True) * jnp.where(
        lax.broadcasted_iota(jnp.int32, (8, 1), 0) == 0, 1.0, 0.0
    )

    def cols_of(k):
        return pl.ds(pl.multiple_of(k * 128, 128), 128)

    def to_owner(k):
        to = lax.rem(e + k, EXP)
        return to, remote(
            acc.at[:, cols_of(lax.rem(to, OWNERS))], ar_a.at[k], ra_s.at[k], ra_r.at[k], (dp, to, t)
        )

    def send_owner(k, c):
        to, copy = to_owner(k)

        @pl.when(to < OWNERS)
        def _():
            copy.start()

        return c

    lax.fori_loop(1, EXP, send_owner, 0)

    def finish(rg, buf, base, two_p, two_m, three_p, three_m, count, dst):
        rg["sum_p"].wait_recv()
        rg["raw_m"].wait_recv()

        def put_lo(rows, v):
            dst[rows, lo] = v

        def put_hi(rows, v):
            dst[rows, hi] = v

        add_rows(
            put_lo,
            (
                lambda r: buf[pl.ds(base(x) + r.start, 32), lo],
                lambda r: two_p[r, :],
                lambda r: three_m[r, :],
            ),
            count,
        )
        rg["sum_m"].wait_recv()
        rg["raw_p"].wait_recv()
        add_rows(
            put_hi,
            (
                lambda r: buf[pl.ds(base(x) + r.start, 32), hi],
                lambda r: two_m[r, :],
                lambda r: three_p[r, :],
            ),
            count,
        )

    finish(ring_a, p1, base_a, a2p, a2m, a3p, a3m, 320, ysum)
    mine = pl.multiple_of(ylo * 160, 160)
    other = pl.multiple_of((1 - ylo) * 160, 160)
    last = remote(ysum.at[pl.ds(other, 160)], ya, yas_sem, yar_sem, ypeer)
    last.start()

    @pl.when(e < OWNERS)
    def _():
        ar_x[x] = acc[:, cols_of(lax.rem(e, OWNERS))]

        def gather(k, c):
            to_owner(k)[1].wait_recv()
            ar_x[x] += ar_a[k]
            return c

        lax.fori_loop(1, EXP, gather, 0)
        for k in (1, 2, 3):
            remote(ar_x.at[x], ar_x.at[x], rx_s.at[k], rx_r.at[k], xdev(k)).start()
        for k in (1, 2, 3):
            src = lax.rem(x + 4 - k, 4)
            remote(ar_x.at[src], ar_x.at[src], rx_s.at[k], rx_r.at[k], xdev(k)).wait_recv()
        ar_y[y] = ar_x[0] + ar_x[1] + ar_x[2] + ar_x[3]
        for k in (1, 2, 3):
            remote(ar_y.at[y], ar_y.at[y], ry_s.at[k], ry_r.at[k], ydev(k)).start()
        for k in (1, 2, 3):
            src = lax.rem(y + 4 - k, 4)
            remote(ar_y.at[src], ar_y.at[src], ry_s.at[k], ry_r.at[k], ydev(k)).wait_recv()
        cols = cols_of(lax.rem(e, OWNERS))
        fin_ref[:, cols] = ar_y[0] + ar_y[1] + ar_y[2] + ar_y[3]

        def hand(k, c):
            to = lax.rem(e + k, EXP)
            remote(fin_ref.at[:, cols], fin_ref.at[:, cols], rc_s.at[k], rc_r.at[k], (dp, to, t)).start()
            return c

        lax.fori_loop(1, EXP, hand, 0)

    finish(ring_b, tb, base_t, b2p, b2m, b3p, b3m, 160, g2_ref)
    last.wait_recv()

    def put_g1(rows, v):
        g1_ref[rows, :] = v

    add_rows(
        put_g1,
        (lambda r: ysum[pl.ds(mine + r.start, 32), :], lambda r: ya[r, :]),
        160,
    )

    def taken(k, c):
        src = lax.rem(e + EXP - k, EXP)

        @pl.when(src < OWNERS)
        def _():
            cols = cols_of(lax.rem(src, OWNERS))
            remote(fin_ref.at[:, cols], fin_ref.at[:, cols], rc_s.at[k], rc_r.at[k], (dp, src, t)).wait_recv()

        return c

    lax.fori_loop(1, EXP, taken, 0)

    def drain(b, c):
        def one(j, c):
            a2a(b, j).wait_send()
            back(b, j).wait_send()
            relay(b, e, j).wait_send()
            return c

        lax.fori_loop(0, 15, one, c)
        relay(b, e, 15).wait_send()
        return c

    lax.fori_loop(0, BATCHES, drain, 0)
    for b in range(BATCHES):
        partial(b).wait_send()
    for q, k in enumerate(chunks):
        send_y(q, k).wait_send()
    for rg in (ring_a, ring_b):
        for copy in rg.values():
            copy.wait_send()
    last.wait_send()

    def drain_owner(k, c):
        to, copy = to_owner(k)

        @pl.when(to < OWNERS)
        def _():
            copy.wait_send()

        return c

    lax.fori_loop(1, EXP, drain_owner, 0)

    @pl.when(e < OWNERS)
    def _():
        for k in (1, 2, 3):
            remote(ar_x.at[x], ar_x.at[x], rx_s.at[k], rx_r.at[k], xdev(k)).wait_send()
            remote(ar_y.at[y], ar_y.at[y], ry_s.at[k], ry_r.at[k], ydev(k)).wait_send()
        cols = cols_of(lax.rem(e, OWNERS))

        def sent(k, c):
            to = lax.rem(e + k, EXP)
            remote(fin_ref.at[:, cols], fin_ref.at[:, cols], rc_s.at[k], rc_r.at[k], (dp, to, t)).wait_send()
            return c

        lax.fori_loop(1, EXP, sent, 0)

    def drain_out(i, c):
        pltpu.make_async_copy(normed.at[i], out_hbm.at[i], out_sem.at[i]).wait()
        return c

    lax.fori_loop(0, IMGS, drain_out, 0)


def local(tokens, cotangent, norm_gain, slot_keys, w_in, w_out):
    V = pltpu.VMEM
    S = pltpu.SemaphoreType.DMA
    any_ = pl.BlockSpec(memory_space=pl.ANY)
    vm = pl.BlockSpec(memory_space=pltpu.VMEM)
    scratch = [
        V((IMGS, TOK, D), BF16), V((IMGS, TOK, D), BF16), V((IMGS, TOK, D), BF16),
        V((D, HID), BF16), V((HID, D), BF16),
        V((IMGS, SLOTS, TOK), F32), V((IMGS, SLOTS, TOK), F32), V((IMGS, TOK, 128), F32),
        V((128, D), BF16), V((ROWS, D), BF16), V((2 * ROWS, D), BF16),
        V((ROWS, D), BF16), V((ROWS, D), BF16), V((D, ROWS), BF16), V((D, ROWS), BF16),
        V((ROWS, HID), BF16), V((ROWS, HID), BF16),
        V((ROWS, D), BF16), V((ROWS, D), BF16), V((ROWS, D), F32), V((ROWS, D), BF16), V((ROWS, D), BF16),
        V((D, HID), BF16), V((D, HID), BF16),
    ]
    scratch += [V((320, HALF), BF16)] * 6
    scratch += [V((160, D), BF16), V((HALF, D), BF16), V((HALF, D), BF16)]
    scratch += [V((160, HALF), BF16)] * 6
    scratch += [
        V((320, D), BF16),
        V((TOK, D), F32), V((96, D), BF16), V((STAT, D), F32), V((8, D), F32),
        V((EXP, STAT, 128), F32), V((4, STAT, 128), F32), V((4, STAT, 128), F32),
    ]
    scratch += [
        S((IMGS,)), S((IMGS,)), S((2,)), S((IMGS,)), S((BATCHES,)),
        S((BATCHES, 15)), S((BATCHES, 15)), S((BATCHES, 16)), S((BATCHES, 16)),
        S((BATCHES,)), S((BATCHES,)), S((BATCHES, 15)), S((BATCHES, 15)),
        S((6,)), S((6,)), S((6,)), S((6,)), S(()), S(()), S((4,)), S((4,)),
        S((EXP,)), S((EXP,)), S((4,)), S((4,)), S((4,)), S((4,)), S((EXP,)), S((EXP,)),
    ]
    out, fin, g1, g2 = pl.pallas_call(
        kernel,
        name="moe_block",
        out_shape=(
            jax.ShapeDtypeStruct((IMGS, TOK, D), BF16),
            jax.ShapeDtypeStruct((STAT, D), F32),
            jax.ShapeDtypeStruct((160, HID), BF16),
            jax.ShapeDtypeStruct((160, HID), BF16),
        ),
        in_specs=[any_, any_, vm, vm, any_, any_],
        out_specs=(any_, vm, vm, vm),
        scratch_shapes=scratch,
        compiler_params=pltpu.CompilerParams(
            collective_id=0, has_side_effects=True, vmem_limit_bytes=67043328
        ),
    )(tokens, cotangent, norm_gain[None], slot_keys.T, w_in, w_out)
    return out, fin[SLOTS], fin[:SLOTS].T, g1[None], g2.T[None]


def solution(mesh):
    images = P(("dp", "expert", "tensor"), None, None)
    return jax.shard_map(
        local,
        mesh=mesh,
        in_specs=(images, images, P(), P(), P("expert", None, "tensor"), P("expert", "tensor", None)),
        out_specs=(images, P(), P(), P("expert", "dp", "tensor"), P("expert", "tensor", "dp")),
        check_vma=False,
    )
```

time: 504 us -> 146 us (0.29)
  waiting for transfers between devices: 232 us -> 0 us
  Pallas kernels: 0 us -> 135 us
  blocking collectives: 118 us -> 0 us
  matrix products: 62.9 us -> 0 us
  starting transfers between devices: 32.3 us -> 0 us
  other arithmetic: 16.2 us -> 0 us
  between operations: 15.7 us -> 0.64 us
  local copies, waits for them, and re-layouts: 24.8 us -> 10.2 us
    psum x1 -> x0, waiting for transfers between devices: 165 us -> none  [local(): lax.psum((gain_term, keys_term), ('dp', 'expert', 'tensor'))]
    pallas_call x0 -> x1, Pallas kernels: none -> 135 us  [local(): pl.pallas_call(kernel, name='moe_block', out_shape=(jax.ShapeDtypeStruct(...]
    psum x1 -> x0, blocking collectives: 79.7 us -> none  [local(): lax.psum((gain_term, keys_term), ('dp', 'expert', 'tensor'))]
    all_to_all x6 -> x0, waiting for transfers between devices: 67.7 us -> none  [the longest x1 19.8 us: summed_on_arrival(): lax.all_to_all(tiles, axis, split_axis=0, concat_axis=0, tiled=True)]
    dot_general x14 -> x0, matrix products: 62.9 us -> none  [the longest x1 10.7 us: mixing_backward(): jnp.einsum('bmn,dn->bmd', grad_logits, keys_wide, precision=lax.Precision...]
    all_to_all x2 -> x0, blocking collectives: 38.3 us -> none  [the longest x1 19.4 us: local(): lax.all_to_all(slot_inputs, 'expert', split_axis=1, concat_axis=0, tiled=...]
    all_to_all x6 -> x0, starting transfers between devices: 31.6 us -> none  [the longest x1 9.97 us: local(): lax.all_to_all(grad_slots, 'expert', split_axis=1, concat_axis=0, tiled=T...]
    reshape x7 -> x0, local copies, waits for them, and re-layouts: 10.7 us -> none  [the longest x2 4.15 us: local(): slot_values.astype(jnp.bfloat16)]
  transfers between devices with their start and end apart: 9 -> 0, of which waited for: 7 -> 0; matrix products, arithmetic and copies ran while one was open for 13% -> 0% of each run, Pallas kernels for 0% -> 0%
where the time goes in v1:
time: 146 us
  Pallas kernels  135 us (92%)
  local copies, waits for them, and re-layouts  10.2 us (7%)
    pallas_call x1, Pallas kernels, local(): pl.pallas_call(kernel, name='moe_block', out_shape=(jax.ShapeDtypeStruct(...  135 us
    unnamed x7, local copies, waits for them, and re-layouts  5.87 us

profile of v1, /device:TPU:1, one launch (start us, length us, event | category | flops | bytes accessed | tf_op | source)
XLA Modules:
  0.0 146.1 jit_solution(1860707055765673909)
XLA Ops:
  0.6 1.3 broadcast_in_dim.9.gain_ref
  1.9 135.3 %moe_block.1 = (bf16[6,256,1280]{2,1,0:T(8,128)(2,1)}, f32[40,1280]{1,0:T(8,128)}, bf16[160,1280]{1,0:T(8,128)(2,1)}, bf16[160,1280]{1,0:T(8,128)(2,1)}) custom-call(bf16[6,256,1280]{2,1,0:T(8,128)(2,1)} %tok_hbm.1, bf16[6,256,1280]{2,1,0:T(8,128)(2,1)} %cot_hbm.1, f32[1,1280]{1,0:T(1,128)} %broadcast_in_dim.9.gain_ref, bf16[32,1280]{1,0:T(8,128)(2,1)} %bitcast.9, ...), custom_call_target="tpu_custom_call" | custom-call | tf_op jit(solution)/shard_map/moe_block/pallas_call | solution.py:694
  137.2 1.6 %slice_bitcast_fusion = f32[1280,32]{0,1:T(8,128)} fusion(f32[40,1280]{1,0:T(8,128)} %get-tuple-element.10), kind=kLoop, calls=%fused_computation | loop fusion | bytes 327680 | tf_op jit(solution)/shard_map/transpose | solution.py:710
  138.8 1.4 slice_reduce_fusion
  140.2 0.0 copy-start.1
  140.2 0.0 copy-start
  140.2 4.4 %copy.14 = bf16[6,256,1280]{2,1,0:T(8,128)(2,1)} copy(bf16[6,256,1280]{2,1,0:T(8,128)(2,1)} %get-tuple-element.18) | data formatting | bytes 7864320
  144.6 0.0 copy-done.1
  144.6 0.8 copy.15
  145.3 0.0 copy-done
  145.4 0.8 copy.16
Async XLA Ops:
  140.2 4.4 %copy-start.1 = (bf16[160,1280]{1,0:T(8,128)(2,1)S(1)}, bf16[160,1280]{1,0:T(8,128)(2,1)}, u32[]{:S(2)}) copy-start(bf16[160,1280]{1,0:T(8,128)(2,1)} %get-tuple-element.11) | copy-start | bytes 1228804
  140.2 5.1 %copy-start = (bf16[160,1280]{1,0:T(8,128)(2,1)S(1)}, bf16[160,1280]{1,0:T(8,128)(2,1)}, u32[]{:S(2)}) copy-start(bf16[160,1280]{1,0:T(8,128)(2,1)} %get-tuple-element.12) | copy-start | bytes 1228804
